TPU v7x, 32 devices: a whole 2x2x4 slice. The times are simulated.
32 devices in a mesh: gy: 8 (over z, y), gz: 4 (over x, core).
Axes of the slice: x: 2, y: 2, z: 4, core: 2. Of those that a mesh axis runs over, the one named last changes fastest.
Arguments:
- tokens: bfloat16 [2, 64, 8, 8, 1024], P(None, None, 'gy', 'gz'), may hold values from -64 to 64
- w_qkv: bfloat16 [1024, 3072], P('gy'), may hold values from -2 to 2
- w_out: bfloat16 [1024, 1024], P('gy'), may hold values from -0.1875 to 0.1875
- bias_x: float32 [16, 127], replicated, may hold values from -4 to 4
- bias_y: float32 [16, 15], replicated, may hold values from -4 to 4
- bias_z: float32 [16, 15], replicated, may hold values from -4 to 4
Outputs:
- mixed: bfloat16 [2, 64, 8, 8, 1024], P(None, None, 'gy', 'gz')
All inputs are finite; a program needn't handle non-finite values.
Results may differ from a plain program's by a relative error of at most 0.0083.
Values may be sent and summed in bfloat16 or wider, within the bound.
A program may use at most 64 MiB of HBM per device.

v0:
```python
import jax
import jax.numpy as jnp
from jax import lax
from jax.sharding import PartitionSpec as P

HEADS = 16
HEAD = 64
einsum_forms = {
    1: ("bxyzhs,bwyzhs->byzhxw", "byzhxw,bwyzhs->bxyzhs"),
    2: ("bxyzhs,bxwzhs->bxzhyw", "bxzhyw,bxwzhs->bxyzhs"),
    3: ("bxyzhs,bxywhs->bxyhzw", "bxyhzw,bxywhs->bxyzhs"),
}


def norm_rows(tokens):
    values = tokens.astype(jnp.float32)
    center = jnp.mean(values, axis=-1, keepdims=True)
    spread = jnp.mean((values - center) ** 2, axis=-1, keepdims=True)
    return ((values - center) * lax.rsqrt(spread + 1e-05)).astype(jnp.bfloat16)


def rel_bias(table):
    length = (table.shape[1] + 1) // 2
    offsets = (
        lax.broadcasted_iota(jnp.int32, (length, length), 0)
        - lax.broadcasted_iota(jnp.int32, (length, length), 1)
        + length
        - 1
    )
    lookup = (
        offsets[:, :, None] == lax.broadcasted_iota(jnp.int32, (1, 1, 2 * length - 1), 2)
    ).astype(jnp.float32)
    return jnp.einsum("hr,ijr->hij", table, lookup, precision=lax.Precision.HIGHEST)


def attend(qkv, table, axis):
    dims = qkv.shape
    features = dims[-1] // 3
    parts = qkv.reshape(dims[:-1] + (3, HEADS, HEAD))
    query = parts[..., 0, :, :]
    keys = parts[..., 1, :, :]
    values = parts[..., 2, :, :]
    score_form, mix_form = einsum_forms[axis]
    scores = jnp.einsum(score_form, query, keys, preferred_element_type=jnp.float32) * HEAD ** (
        -0.5
    ) + rel_bias(table)
    scores = scores - jnp.max(scores, axis=-1, keepdims=True)
    expo = jnp.exp(scores)
    weights = (expo / jnp.sum(expo, axis=-1, keepdims=True)).astype(jnp.bfloat16)
    mixed = jnp.einsum(mix_form, weights, values, preferred_element_type=jnp.float32)
    return mixed.reshape(dims[:-1] + (features,)).astype(jnp.bfloat16)


def return_y(result):
    return lax.all_to_all(result, "gy", split_axis=2, concat_axis=1, tiled=True)


def return_z(result):
    return lax.all_to_all(result, "gz", split_axis=3, concat_axis=1, tiled=True)


def shards(tokens, w_qkv, w_out, bias_x, bias_y, bias_z):
    samples, depth, rows_y, rows_z, features = tokens.shape
    normed = norm_rows(tokens)
    gathered = lax.all_gather(w_qkv, "gy", axis=0, tiled=True)

    def project(inputs):
        product = jnp.dot(
            inputs.reshape(-1, features), gathered, preferred_element_type=jnp.float32
        )
        return product.astype(jnp.bfloat16).reshape(inputs.shape[:-1] + (3 * features,))

    along_x = attend(project(normed), bias_x, 1)
    along_y = return_y(
        attend(
            project(lax.all_to_all(normed, "gy", split_axis=1, concat_axis=2, tiled=True)),
            bias_y,
            2,
        )
    )
    along_z = return_z(
        attend(
            project(lax.all_to_all(normed, "gz", split_axis=1, concat_axis=3, tiled=True)),
            bias_z,
            3,
        )
    )
    summed = along_x.astype(jnp.float32) + along_y.astype(jnp.float32) + along_z.astype(jnp.float32)
    summed = summed.astype(jnp.bfloat16).reshape(-1, features)
    residual = tokens.reshape(-1, features).astype(jnp.float32)
    result = residual + jnp.dot(
        summed, lax.all_gather(w_out, "gy", axis=0, tiled=True), preferred_element_type=jnp.float32
    )
    return result.astype(jnp.bfloat16).reshape(tokens.shape)


def solution(mesh):
    placed = (P(None, None, "gy", "gz", None), P("gy", None), P("gy", None), P(), P(), P())
    return jax.shard_map(
        shards,
        mesh=mesh,
        in_specs=placed,
        out_specs=P(None, None, "gy", "gz", None),
        check_vma=False,
    )
```

profile of v0, /device:TPU:0, one launch (start us, length us, event | category | flops | bytes accessed | tf_op | source)
XLA Modules:
  0.0 212.9 jit_solution(13488122357055576503)
XLA Ops:
  6.5 0.7 all-gather.3.cloned.1.call-update
  7.3 1.6 convert_reduce_fusion
  8.9 0.0 copy-start.11
  8.9 1.9 multiply_reduce_fusion
  10.8 0.1 add_rsqrt_fusion
  10.9 0.0 copy-start.12
  10.9 1.4 multiply_convert_fusion
  12.3 4.2 %all-to-all-start.2 = ((bf16[2,64,1,2,1024]{4,3,2,0,1:T(2,128)(2,1)}), bf16[2,64,1,2,1024]{4,3,2,0,1:T(2,128)(2,1)S(1)}, u32[]{:S(2)}, u32[]{:S(2)}) async-start(bf16[2,64,1,2,1024]{4,3,2,0,1:T(2,128)(2,1)} %multiply_convert_fusion), calls=%async_computation.2 | async-start | bytes 1048576 | tf_op jit(solution)/shard_map/all_to_all | solution.py:83
  16.6 0.7 all-gather.5.cloned.1.call-update
  17.3 8.1 %all-to-all-done.2 = bf16[2,64,1,2,1024]{4,3,2,0,1:T(2,128)(2,1)S(1)} async-done(((bf16[2,64,1,2,1024]{4,3,2,0,1:T(2,128)(2,1)}), bf16[2,64,1,2,1024]{4,3,2,0,1:T(2,128)(2,1)S(1)}, u32[]{:S(2)}, u32[]{:S(2)}) %all-to-all-start.2) | async-done | bytes 524320 | tf_op jit(solution)/shard_map/all_to_all | solution.py:83
  25.4 6.5 %all-to-all-start = ((bf16[2,64,1,2,1024]{4,3,2,0,1:T(2,128)(2,1)}), bf16[2,64,1,2,1024]{4,3,2,0,1:T(2,128)(2,1)S(1)}, u32[]{:S(2)}, u32[]{:S(2)}) async-start(bf16[2,64,1,2,1024]{4,3,2,0,1:T(2,128)(2,1)} %multiply_convert_fusion), calls=%async_computation | async-start | bytes 1048576 | tf_op jit(solution)/shard_map/all_to_all | solution.py:76
  31.9 0.2 convolution_bitcast_fusion.1
  32.1 1.4 copy.77
  33.5 0.1 copy.88
  33.6 0.2 convolution_bitcast_fusion
  33.8 0.1 copy.97
  33.9 1.0 reshape.177
  35.0 3.2 %fusion.11 = f32[16,64,64]{2,0,1:T(8,128)S(1)} fusion(s32[64,64]{1,0:T(8,128)S(1)} %subtract_add_fusion, f32[16,127]{1,0:T(8,128)S(1)} %copy-done), kind=kOutput, calls=%fused_computation.29 | convolution fusion | flops 100397056 | bytes 286656 | tf_op jit(solution)/shard_map/hr,ijr->hij/dot_general | solution.py:33
  38.1 1.1 copy.81
  39.2 0.6 copy_convert_fusion
  39.8 0.1 copy.76
  39.9 1.7 reshape.187
  41.6 0.5 copy.174
  42.2 0.2 reshape.182
  42.4 17.7 %all-to-all-done = bf16[2,64,1,2,1024]{4,3,2,0,1:T(2,128)(2,1)S(1)} async-done(((bf16[2,64,1,2,1024]{4,3,2,0,1:T(2,128)(2,1)}), bf16[2,64,1,2,1024]{4,3,2,0,1:T(2,128)(2,1)S(1)}, u32[]{:S(2)}, u32[]{:S(2)}) %all-to-all-start) | async-done | bytes 524320 | tf_op jit(solution)/shard_map/all_to_all | solution.py:76
  60.1 0.5 copy.175
  60.5 1.0 reshape.181
  61.5 60.6 %all-gather.3.cloned.1.call-done = bf16[1024,3072]{1,0:T(8,128)(2,1)} async-done(((bf16[128,3072]{1,0:T(8,128)(2,1)}), bf16[1024,3072]{1,0:T(8,128)(2,1)}) %all-gather.3.cloned.1.call-update) | async-done | bytes 6291472 | tf_op jit(solution)/shard_map/all_gather | solution.py:65
  122.1 5.8 %convolution_convert_fusion = bf16[256,3072]{1,0:T(8,128)(2,1)} fusion(bf16[256,1024]{1,0:T(8,128)(2,1)S(1)} %reshape.182, bf16[1024,3072]{1,0:T(8,128)(2,1)} %all-gather.3.cloned.1.call-done), kind=kOutput, calls=%fused_computation.3 | convolution fusion | flops 1611399168 | bytes 8388608 | tf_op jit(solution)/shard_map/dot_general | solution.py:68
  127.9 3.6 %reshape_reshape.11 = bf16[2,16,1,8,3,16,64]{6,5,4,3,1,0,2:T(8,128)(2,1)S(1)} reshape(bf16[256,3072]{1,0:T(8,128)(2,1)} %convolution_convert_fusion) | data formatting | bytes 3145728 | tf_op jit(solution)/shard_map/reshape;reshape | solution.py:39
  131.6 0.0 copy-start.10
  131.6 2.1 fusion.36
  133.7 5.9 %convolution_convert_fusion.1 = bf16[256,3072]{1,0:T(8,128)(2,1)} fusion(bf16[256,1024]{1,0:T(8,128)(2,1)S(1)} %copy-done.10, bf16[1024,3072]{1,0:T(8,128)(2,1)} %all-gather.3.cloned.1.call-done), kind=kOutput, calls=%fused_computation.4 | convolution fusion | flops 1611399168 | bytes 8388608 | tf_op jit(solution)/shard_map/dot_general | solution.py:68
  139.6 3.0 %fusion.37 = (f32[2,16,16,8]{3,2,1,0:T(8,128)S(1)}, f32[2,16,16,8,8]{3,4,2,1,0:T(8,128)}) fusion(f32[16,8,8]{1,2,0:T(8,128)S(1)} %copy.97, bf16[2,16,1,8,1,16,64]{6,5,4,3,1,0,2:T(8,128)(2,1)S(1)} %copy-done.8, bf16[2,16,1,8,1,16,64]{6,5,4,3,1,0,2:T(8,128)(2,1)S(1)} %copy-done.7), kind=kOutput, calls=%fused_computation.79 | convolution fusion | flops 4325383 | bytes 1200128 | tf_op jit(solution)/shard_map/sub | solution.py:47
  142.7 3.6 %reshape_reshape.10 = bf16[2,8,8,2,3,16,64]{6,5,4,3,2,1,0:T(8,128)(2,1)S(1)} reshape(bf16[256,3072]{1,0:T(8,128)(2,1)} %convolution_convert_fusion.1) | data formatting | bytes 3145728 | tf_op jit(solution)/shard_map/reshape;reshape | solution.py:39
  146.3 2.7 %fusion.9 = bf16[2,16,1,8,16,64]{5,3,4,1,0,2:T(8,128)(2,1)S(1)} fusion(f32[2,16,16,8,8]{3,4,2,1,0:T(8,128)} %get-tuple-element.15, bf16[2,16,1,8,1,16,64]{6,5,4,3,1,0,2:T(8,128)(2,1)} %get-tuple-element.11, f32[2,16,16,8]{3,2,1,0:T(8,128)S(1)} %get-tuple-element.14), kind=kOutput, calls=%fused_computation.26 | convolution fusion | flops 4521984 | bytes 1196032 | tf_op jit(solution)/shard_map/bxyhzw,bxywhs->bxyzhs/dot_general | solution.py:50
  149.1 1.3 copy.108
  150.4 2.6 %reshape.198 = bf16[2,16,1,8,1024]{4,1,0,2,3:T(8,128)(2,1)} reshape(bf16[2,16,1,8,16,64]{5,4,1,0,3,2:T(8,128)(2,1)} %copy.108) | data formatting | bytes 1048576 | tf_op jit(solution)/shard_map/convert_element_type | solution.py:51
  153.0 4.4 %all-to-all-start.3 = ((bf16[2,16,1,8,1024]{4,1,0,2,3:T(8,128)(2,1)}), bf16[2,16,1,8,1024]{4,1,0,2,3:T(8,128)(2,1)}, u32[]{:S(2)}, u32[]{:S(2)}) async-start(bf16[2,16,1,8,1024]{4,1,0,2,3:T(8,128)(2,1)} %reshape.198), calls=%async_computation.3 | async-start | bytes 1048576 | tf_op jit(solution)/shard_map/all_to_all | solution.py:59
  157.3 2.2 %fusion.34 = (bf16[2,8,8,2,1,16,64]{6,5,4,3,2,1,0:T(8,128)(2,1)}, bf16[2,8,8,2,1,16,64]{6,5,4,3,2,1,0:T(8,128)(2,1)}, bf16[2,8,8,2,1,16,64]{6,5,4,3,2,1,0:T(8,128)(2,1)}) fusion(bf16[2,8,8,2,3,16,64]{6,5,4,3,2,1,0:T(8,128)(2,1)S(1)} %reshape_reshape.10), kind=kLoop, calls=%fused_computation.76 | loop fusion | bytes 3145728 | tf_op jit(solution)/shard_map/slice | solution.py:42
  159.6 3.4 %fusion.39 = (f32[2,8,2,16,8]{4,3,2,1,0:T(8,128)S(1)}, f32[2,8,2,16,8,8]{4,5,3,2,1,0:T(8,128)S(1)}) fusion(f32[16,8,8]{1,2,0:T(8,128)S(1)} %copy.88, bf16[2,8,8,2,1,16,64]{6,5,4,3,2,1,0:T(8,128)(2,1)} %get-tuple-element.7, bf16[2,8,8,2,1,16,64]{6,5,4,3,2,1,0:T(8,128)(2,1)} %get-tuple-element.6), kind=kOutput, calls=%fused_computation.81 | convolution fusion | flops 4325383 | bytes 1200128 | tf_op jit(solution)/shard_map/sub | solution.py:47
  163.0 6.0 %convolution_convert_fusion.2 = bf16[256,3072]{1,0:T(8,128)(2,1)} fusion(bf16[256,1024]{1,0:T(8,128)(2,1)S(1)} %copy-done.9, bf16[1024,3072]{1,0:T(8,128)(2,1)} %all-gather.3.cloned.1.call-done), kind=kOutput, calls=%fused_computation.5 | convolution fusion | flops 1611399168 | bytes 8388608 | tf_op jit(solution)/shard_map/dot_general | solution.py:68
  168.9 0.9 fusion.8
  169.9 0.2 copy.107
  170.1 1.4 reshape.197
  171.5 3.6 %reshape_reshape.9 = bf16[2,64,1,2,3,16,64]{6,5,4,3,1,0,2:T(8,128)(2,1)S(1)} reshape(bf16[256,3072]{1,0:T(8,128)(2,1)} %convolution_convert_fusion.2) | data formatting | bytes 3145728 | tf_op jit(solution)/shard_map/reshape;reshape | solution.py:39
  175.1 1.9 fusion.35
  177.0 2.3 %copy.111 = bf16[2,64,1,2,1,16,64]{1,6,5,3,0,4,2:T(8,128)(2,1)S(1)} copy(bf16[2,64,1,2,1,16,64]{6,5,4,3,1,0,2:T(8,128)(2,1)} %get-tuple-element.8) | data formatting | bytes 1048576
  179.4 0.0 all-to-all-done.3
  179.4 4.4 %all-to-all-start.1 = ((bf16[2,8,8,2,1024]{4,3,1,0,2:T(2,128)(2,1)}), bf16[2,8,8,2,1024]{4,3,1,0,2:T(2,128)(2,1)}, u32[]{:S(2)}, u32[]{:S(2)}) async-start(bf16[2,8,8,2,1024]{4,3,1,0,2:T(2,128)(2,1)} %reshape.197), calls=%async_computation.1 | async-start | bytes 1048576 | tf_op jit(solution)/shard_map/all_to_all | solution.py:55
  183.8 3.7 %fusion.38 = (f32[2,2,16,64]{3,2,1,0:T(8,128)S(1)}, f32[2,2,16,64,64]{3,4,2,1,0:T(8,128)}) fusion(f32[16,64,64]{1,2,0:T(8,128)} %copy.81, bf16[2,64,1,2,1,16,64]{6,5,4,3,1,0,2:T(8,128)(2,1)S(1)} %copy-done.4, bf16[2,64,1,2,1,16,64]{6,5,4,3,1,0,2:T(8,128)(2,1)S(1)} %copy-done.5), kind=kOutput, calls=%fused_computation.80 | convolution fusion | flops 34603072 | bytes 2375680 | tf_op jit(solution)/shard_map/sub | solution.py:47
  187.5 3.4 %convert_bitcast_fusion = f32[2,64,1,2,16,64]{1,5,4,3,0,2:T(8,128)} fusion(f32[2,2,16,64,64]{3,4,2,1,0:T(8,128)} %get-tuple-element.17, bf16[2,64,1,2,1,16,64]{1,6,5,3,0,4,2:T(8,128)(2,1)S(1)} %copy.111, f32[2,2,16,64]{3,2,1,0:T(8,128)S(1)} %get-tuple-element.16), kind=kOutput, calls=%fused_computation.6 | convolution fusion | flops 34603008 | bytes 2637824 | tf_op jit(solution)/shard_map/byzhxw,bwyzhs->bxyzhs/dot_general | solution.py:50
  190.9 3.1 %copy.83 = f32[2,64,1,2,16,64]{5,4,3,1,0,2:T(8,128)S(1)} copy(f32[2,64,1,2,16,64]{1,5,4,3,0,2:T(8,128)} %convert_bitcast_fusion) | data formatting | bytes 2097152 | tf_op jit(solution)/shard_map/convert_element_type | solution.py:88
  194.0 0.6 reshape.188
  194.5 1.1 copy.101
  195.6 0.1 convert_bitcast_fusion.1
  195.7 0.8 copy.102
  196.6 1.8 reshape.190
  198.3 0.3 all-to-all-done.1
  198.7 1.5 convert_bitcast_fusion.2
  200.2 0.1 copy.92
  200.2 1.7 reshape.189
  201.9 3.1 %fusion.10 = bf16[256,1024]{1,0:T(8,128)(2,1)S(1)} fusion(f32[256,1024]{1,0:T(8,128)S(1)} %copy-done.3, bf16[1024,1024]{1,0:T(8,128)(2,1)} %all-gather.5.cloned.1.call-done, f32[256,1024]{1,0:T(8,128)} %reshape.190, f32[256,1024]{1,0:T(8,128)S(1)} %reshape.188, f32[256,1024]{1,0:T(8,128)} %reshape.189), kind=kOutput, calls=%fused_computation.28 | convolution fusion | flops 538181632 | bytes 6815744 | tf_op jit(solution)/shard_map/dot_general | solution.py:91
  205.0 1.0 reshape.186
  (29 shorter events, 0.1 us)
Async XLA Ops:
  6.5 28.4 %copy-start = (f32[16,127]{1,0:T(8,128)S(1)}, f32[16,127]{1,0:T(8,128)}, u32[]{:S(2)}) copy-start(f32[16,127]{1,0:T(8,128)} %param.9) | copy-start | bytes 24388
  6.5 4.3 %copy-start.2 = (bf16[2,64,1,2,1024]{4,3,2,1,0:T(2,128)(2,1)S(1)}, bf16[2,64,1,2,1024]{4,3,2,1,0:T(2,128)(2,1)}, u32[]{:S(2)}) copy-start(bf16[2,64,1,2,1024]{4,3,2,1,0:T(2,128)(2,1)} %param.6) | copy-start | bytes 1572868
  6.5 115.6 %all-gather.3.cloned.1.call-start = ((), (), s32[]{:S(2)}) async-start(), calls=%async_computation.4 | async-start | bytes 7077888 | tf_op jit(solution)/shard_map/all_gather | solution.py:65
  8.9 23.0 %copy-start.11 = (f32[16,15]{1,0:T(8,128)S(1)}, f32[16,15]{1,0:T(8,128)}, u32[]{:S(2)}) copy-start(f32[16,15]{1,0:T(8,128)} %param.10) | copy-start | bytes 2884
  10.9 22.7 %copy-start.12 = (f32[16,15]{1,0:T(8,128)S(1)}, f32[16,15]{1,0:T(8,128)}, u32[]{:S(2)}) copy-start(f32[16,15]{1,0:T(8,128)} %param.11) | copy-start | bytes 2884
  12.3 13.1 %all-to-all-start.2 = ((bf16[2,64,1,2,1024]{4,3,2,0,1:T(2,128)(2,1)}), bf16[2,64,1,2,1024]{4,3,2,0,1:T(2,128)(2,1)S(1)}, u32[]{:S(2)}, u32[]{:S(2)}) async-start(bf16[2,64,1,2,1024]{4,3,2,0,1:T(2,128)(2,1)} %multiply_convert_fusion), calls=%async_computation.2 | async-start | bytes 1048576 | tf_op jit(solution)/shard_map/all_to_all | solution.py:83
  16.6 185.4 %all-gather.5.cloned.1.call-start = ((), (), s32[]{:S(2)}) async-start(), calls=%async_computation.5 | async-start | bytes 2359296 | tf_op jit(solution)/shard_map/all_gather | solution.py:92
  25.4 34.7 %all-to-all-start = ((bf16[2,64,1,2,1024]{4,3,2,0,1:T(2,128)(2,1)}), bf16[2,64,1,2,1024]{4,3,2,0,1:T(2,128)(2,1)S(1)}, u32[]{:S(2)}, u32[]{:S(2)}) async-start(bf16[2,64,1,2,1024]{4,3,2,0,1:T(2,128)(2,1)} %multiply_convert_fusion), calls=%async_computation | async-start | bytes 1048576 | tf_op jit(solution)/shard_map/all_to_all | solution.py:76
  131.6 2.1 %copy-start.10 = (bf16[256,1024]{1,0:T(8,128)(2,1)S(1)}, bf16[256,1024]{1,0:T(8,128)(2,1)}, u32[]{:S(2)}) copy-start(bf16[256,1024]{1,0:T(8,128)(2,1)} %reshape.181) | copy-start | bytes 1572868
  133.7 5.9 %copy-start.7 = (bf16[2,16,1,8,1,16,64]{6,5,4,3,1,0,2:T(8,128)(2,1)S(1)}, bf16[2,16,1,8,1,16,64]{6,5,4,3,1,0,2:T(8,128)(2,1)}, u32[]{:S(2)}) copy-start(bf16[2,16,1,8,1,16,64]{6,5,4,3,1,0,2:T(8,128)(2,1)} %get-tuple-element.12) | copy-start | bytes 1572868
  133.7 5.9 %copy-start.8 = (bf16[2,16,1,8,1,16,64]{6,5,4,3,1,0,2:T(8,128)(2,1)S(1)}, bf16[2,16,1,8,1,16,64]{6,5,4,3,1,0,2:T(8,128)(2,1)}, u32[]{:S(2)}) copy-start(bf16[2,16,1,8,1,16,64]{6,5,4,3,1,0,2:T(8,128)(2,1)} %get-tuple-element.13) | copy-start | bytes 1572868
  153.0 26.4 %all-to-all-start.3 = ((bf16[2,16,1,8,1024]{4,1,0,2,3:T(8,128)(2,1)}), bf16[2,16,1,8,1024]{4,1,0,2,3:T(8,128)(2,1)}, u32[]{:S(2)}, u32[]{:S(2)}) async-start(bf16[2,16,1,8,1024]{4,1,0,2,3:T(8,128)(2,1)} %reshape.198), calls=%async_computation.3 | async-start | bytes 1048576 | tf_op jit(solution)/shard_map/all_to_all | solution.py:59
  159.6 3.4 %copy-start.9 = (bf16[256,1024]{1,0:T(8,128)(2,1)S(1)}, bf16[256,1024]{1,0:T(8,128)(2,1)}, u32[]{:S(2)}) copy-start(bf16[256,1024]{1,0:T(8,128)(2,1)} %reshape.177) | copy-start | bytes 1572868
  163.0 6.0 %copy-start.6 = (bf16[2,8,8,2,1,16,64]{6,5,4,3,2,1,0:T(8,128)(2,1)S(1)}, bf16[2,8,8,2,1,16,64]{6,5,4,3,2,1,0:T(8,128)(2,1)}, u32[]{:S(2)}) copy-start(bf16[2,8,8,2,1,16,64]{6,5,4,3,2,1,0:T(8,128)(2,1)} %get-tuple-element.5) | copy-start | bytes 1572868
  177.0 6.8 %copy-start.4 = (bf16[2,64,1,2,1,16,64]{6,5,4,3,1,0,2:T(8,128)(2,1)S(1)}, bf16[2,64,1,2,1,16,64]{6,5,4,3,1,0,2:T(8,128)(2,1)}, u32[]{:S(2)}) copy-start(bf16[2,64,1,2,1,16,64]{6,5,4,3,1,0,2:T(8,128)(2,1)} %get-tuple-element.9) | copy-start | bytes 1572868
  177.0 6.8 %copy-start.5 = (bf16[2,64,1,2,1,16,64]{6,5,4,3,1,0,2:T(8,128)(2,1)S(1)}, bf16[2,64,1,2,1,16,64]{6,5,4,3,1,0,2:T(8,128)(2,1)}, u32[]{:S(2)}) copy-start(bf16[2,64,1,2,1,16,64]{6,5,4,3,1,0,2:T(8,128)(2,1)} %get-tuple-element.10) | copy-start | bytes 1572868
  179.4 19.3 %all-to-all-start.1 = ((bf16[2,8,8,2,1024]{4,3,1,0,2:T(2,128)(2,1)}), bf16[2,8,8,2,1024]{4,3,1,0,2:T(2,128)(2,1)}, u32[]{:S(2)}, u32[]{:S(2)}) async-start(bf16[2,8,8,2,1024]{4,3,1,0,2:T(2,128)(2,1)} %reshape.197), calls=%async_computation.1 | async-start | bytes 1048576 | tf_op jit(solution)/shard_map/all_to_all | solution.py:55
  200.2 1.8 copy-start.3
  201.9 4.1 %copy-start.1 = (f32[16,127]{1,0:T(8,128)S(1)}, f32[16,127]{1,0:T(8,128)}, u32[]{:S(2)}) copy-start(f32[16,127]{1,0:T(8,128)} %param.9) | copy-start | bytes 24388
Sparse Core Ops, SparseCore 0:
  9.5 112.5 all-gather.2
  124.3 47.2 all-gather.4
where the time goes:
time: 214 us; the launch traced here: 213 us
  waiting for transfers between devices  88.1 us (41%)
  local copies, waits for them, and re-layouts  42.8 us (20%)
  matrix products  41.5 us (19%)
  starting transfers between devices  19.5 us (9%)
  between operations  13.7 us (6%)
  other arithmetic  7.17 us (3%)
    all_gather x1, waiting for transfers between devices, shards(): gathered = lax.all_gather(w_qkv, 'gy', axis=0, tiled=True)  60.6 us
    all_to_all x1, waiting for transfers between devices, shards(): lax.all_to_all(normed, 'gy', split_axis=1, concat_axis=2, tiled=True)  17.7 us
    dot_general x3, matrix products, project(): jnp.dot(inputs.reshape(-1, features), gathered, preferred_element_type=jn...  17.7 us
    another operation x3, local copies, waits for them, and re-layouts, attend(): parts = qkv.reshape(dims[:-1] + (3, HEADS, HEAD))  10.9 us
    sub x3, matrix products, attend(): scores = scores - jnp.max(scores, axis=-1, keepdims=True)  10.1 us
    all_to_all x1, waiting for transfers between devices, shards(): lax.all_to_all(normed, 'gz', split_axis=1, concat_axis=3, tiled=True)  8.07 us
    dot_general x3, matrix products, attend(): jnp.einsum(mix_form, weights, values, preferred_element_type=jnp.float32)  7.03 us
    all_to_all x1, starting transfers between devices, shards(): lax.all_to_all(normed, 'gy', split_axis=1, concat_axis=2, tiled=True)  6.52 us
  transfers between devices with their start and end apart: 6, of which 4 were waited for; matrix products, arithmetic and copies ran while one was open for 41% of the time, Pallas kernels for 0%

commit v1 on v0

--- a/solution.py
+++ b/solution.py
@@ -62,7 +62,9 @@
 def shards(tokens, w_qkv, w_out, bias_x, bias_y, bias_z):
     samples, depth, rows_y, rows_z, features = tokens.shape
     normed = norm_rows(tokens)
-    gathered = lax.all_gather(w_qkv, "gy", axis=0, tiled=True)
+    gathered = jnp.concatenate(
+        lax.all_to_all(jnp.stack([w_qkv] * lax.axis_size("gy")), "gy", 0, 0), axis=0
+    )
 
     def project(inputs):
         product = jnp.dot(

time: 214 us -> 309 us (1.44)
  waiting for transfers between devices: 88.1 us -> 153 us
  blocking collectives: 0 us -> 32.6 us
  starting transfers between devices: 19.5 us -> 13.9 us
    all_to_all x2 -> x1, waiting for transfers between devices: 25.7 us -> 152 us  [shards(): lax.all_to_all(jnp.stack([w_qkv] * lax.axis_size('gy')), 'gy', 0, 0)]
    all_gather x1 -> x0, waiting for transfers between devices: 60.6 us -> none  [shards(): gathered = lax.all_gather(w_qkv, 'gy', axis=0, tiled=True)]
    all_to_all x0 -> x2, blocking collectives: none -> 32.6 us  [the longest x1 19.7 us: shards(): lax.all_to_all(normed, 'gy', split_axis=1, concat_axis=2, tiled=True)]
    all_to_all x2 -> x1, starting transfers between devices: 10.8 us -> 4.89 us  [shards(): lax.all_to_all(jnp.stack([w_qkv] * lax.axis_size('gy')), 'gy', 0, 0)]
    another operation x0 -> x1, local copies, waits for them, and re-layouts: none -> 3.45 us  [shards(): jnp.stack([w_qkv] * lax.axis_size('gy'))]
  transfers between devices with their start and end apart: 6 -> 4, of which waited for: 4 -> 2; matrix products, arithmetic and copies ran while one was open for 41% -> 27% of each run, Pallas kernels for 0% -> 0%
where the time goes in v1:
time: 309 us; the launch traced here: 308 us
  waiting for transfers between devices  153 us (50%)
  local copies, waits for them, and re-layouts  44.4 us (14%)
  matrix products  42.8 us (14%)
  blocking collectives  32.6 us (11%)
  starting transfers between devices  13.9 us (4%)
  between operations  13.8 us (4%)
  other arithmetic  7.47 us (2%)
    all_to_all x1, waiting for transfers between devices, shards(): lax.all_to_all(jnp.stack([w_qkv] * lax.axis_size('gy')), 'gy', 0, 0)  152 us
    all_to_all x1, blocking collectives, shards(): lax.all_to_all(normed, 'gy', split_axis=1, concat_axis=2, tiled=True)  19.7 us
    dot_general x3, matrix products, project(): jnp.dot(inputs.reshape(-1, features), gathered, preferred_element_type=jn...  17.4 us
    all_to_all x1, blocking collectives, shards(): lax.all_to_all(normed, 'gz', split_axis=1, concat_axis=3, tiled=True)  12.9 us
    sub x3, matrix products, attend(): scores = scores - jnp.max(scores, axis=-1, keepdims=True)  11.6 us
    another operation x3, local copies, waits for them, and re-layouts, attend(): parts = qkv.reshape(dims[:-1] + (3, HEADS, HEAD))  10.9 us
    dot_general x3, matrix products, attend(): jnp.einsum(mix_form, weights, values, preferred_element_type=jnp.float32)  7.02 us
    slice x3, local copies, waits for them, and re-layouts, attend(): values = parts[..., 2, :, :]  6.37 us
  transfers between devices with their start and end apart: 4, of which 2 were waited for; matrix products, arithmetic and copies ran while one was open for 27% of the time, Pallas kernels for 0%

profile of v1, /device:TPU:0, one launch (start us, length us, event | category | flops | bytes accessed | tf_op | source)
XLA Modules:
  0.0 307.5 jit_solution(5048563156827702463)
XLA Ops:
  6.5 1.6 convert_reduce_fusion
  8.1 0.0 copy-start.7
  8.2 2.0 multiply_reduce_fusion
  10.1 0.1 add_rsqrt_fusion
  10.2 1.7 multiply_convert_fusion
  11.9 12.9 %all_to_all.53 = bf16[2,64,1,2,1024]{4,3,2,0,1:T(2,128)(2,1)S(1)} all-to-all(bf16[2,64,1,2,1024]{4,3,2,0,1:T(2,128)(2,1)S(1)} %multiply_convert_fusion), channel_id=1, replica_groups=mesh['gy'=8,'gz'=4] {'gz'}, dimensions={1} | all-to-all | bytes 1048576 | tf_op jit(solution)/shard_map/all_to_all | solution.py:85
  24.7 19.7 %all_to_all.54 = bf16[2,64,1,2,1024]{4,3,2,0,1:T(2,128)(2,1)S(1)} all-to-all(bf16[2,64,1,2,1024]{4,3,2,0,1:T(2,128)(2,1)S(1)} %multiply_convert_fusion), channel_id=1, replica_groups=mesh['gy'=8,'gz'=4] {'gy'}, dimensions={1} | all-to-all | bytes 1048576 | tf_op jit(solution)/shard_map/all_to_all | solution.py:78
  44.5 3.4 %stack.2 = bf16[8,128,3072]{2,1,0:T(8,128)(2,1)} broadcast(bf16[128,3072]{1,0:T(8,128)(2,1)S(1)} %copy-done.7), dimensions={1,2} | broadcast | bytes 7077888 | tf_op jit(solution)/shard_map/stack | solution.py:66
  47.9 4.9 %all-to-all-start = ((bf16[8,128,3072]{2,1,0:T(8,128)(2,1)}), bf16[8,128,3072]{2,1,0:T(8,128)(2,1)}, u32[]{:S(2)}, u32[]{:S(2)}) async-start(bf16[8,128,3072]{2,1,0:T(8,128)(2,1)} %stack.2), calls=%async_computation | async-start | bytes 12582912 | tf_op jit(solution)/shard_map/all_to_all | solution.py:66
  52.8 0.2 all-gather.2.cloned.1.call-start
  53.0 0.5 all-gather.2.cloned.1.call-update
  53.6 0.0 copy-start.2
  53.6 0.4 copy.77
  54.0 0.2 convolution_bitcast_fusion.1
  54.2 0.1 copy.88
  54.3 0.2 convolution_bitcast_fusion
  54.5 0.1 copy.97
  54.6 1.0 reshape.182
  55.6 0.0 copy-done
  55.6 3.2 %fusion.11 = f32[16,64,64]{2,0,1:T(8,128)S(1)} fusion(s32[64,64]{1,0:T(8,128)S(1)} %subtract_add_fusion, f32[16,127]{1,0:T(8,128)S(1)} %copy-done), kind=kOutput, calls=%fused_computation.29 | convolution fusion | flops 100397056 | bytes 286656 | tf_op jit(solution)/shard_map/hr,ijr->hij/dot_general | solution.py:33
  58.8 1.1 copy.81
  59.9 0.6 copy_convert_fusion
  60.5 0.1 copy.76
  60.5 1.7 reshape.193
  62.3 0.5 copy.174
  62.8 0.2 reshape.188
  63.0 0.5 copy.175
  63.5 0.2 reshape.187
  63.7 151.6 %all-to-all-done = bf16[8,128,3072]{2,1,0:T(8,128)(2,1)} async-done(((bf16[8,128,3072]{2,1,0:T(8,128)(2,1)}), bf16[8,128,3072]{2,1,0:T(8,128)(2,1)}, u32[]{:S(2)}, u32[]{:S(2)}) %all-to-all-start) | async-done | bytes 6291488 | tf_op jit(solution)/shard_map/all_to_all | solution.py:66
  215.3 5.8 %convolution_convert_fusion.1 = bf16[256,3072]{1,0:T(8,128)(2,1)} fusion(bf16[256,1024]{1,0:T(8,128)(2,1)S(1)} %reshape.187, bf16[1024,3072]{1,0:T(8,128)(2,1)} %bitcast), kind=kOutput, calls=%fused_computation.4 | convolution fusion | flops 1611399168 | bytes 8388608 | tf_op jit(solution)/shard_map/dot_general | solution.py:70
  221.2 5.8 %convolution_convert_fusion = bf16[256,3072]{1,0:T(8,128)(2,1)} fusion(bf16[256,1024]{1,0:T(8,128)(2,1)S(1)} %reshape.188, bf16[1024,3072]{1,0:T(8,128)(2,1)} %bitcast), kind=kOutput, calls=%fused_computation.3 | convolution fusion | flops 1611399168 | bytes 8388608 | tf_op jit(solution)/shard_map/dot_general | solution.py:70
  226.9 3.6 %reshape_reshape.11 = bf16[2,16,1,8,3,16,64]{6,5,4,3,1,0,2:T(8,128)(2,1)S(1)} reshape(bf16[256,3072]{1,0:T(8,128)(2,1)} %convolution_convert_fusion) | data formatting | bytes 3145728 | tf_op jit(solution)/shard_map/reshape;reshape | solution.py:39
  230.6 2.2 fusion.36
  232.7 4.6 %fusion.37 = (f32[2,16,16,8]{3,2,1,0:T(8,128)S(1)}, f32[2,16,16,8,8]{3,4,2,1,0:T(8,128)}) fusion(f32[16,8,8]{1,2,0:T(8,128)S(1)} %copy.97, bf16[2,16,1,8,1,16,64]{6,5,4,3,1,0,2:T(8,128)(2,1)} %get-tuple-element.13, bf16[2,16,1,8,1,16,64]{6,5,4,3,1,0,2:T(8,128)(2,1)} %get-tuple-element.12), kind=kOutput, calls=%fused_computation.79 | convolution fusion | flops 4325383 | bytes 1200128 | tf_op jit(solution)/shard_map/sub | solution.py:47
  237.3 3.6 %reshape_reshape.10 = bf16[2,8,8,2,3,16,64]{6,5,4,3,2,1,0:T(8,128)(2,1)S(1)} reshape(bf16[256,3072]{1,0:T(8,128)(2,1)} %convolution_convert_fusion.1) | data formatting | bytes 3145728 | tf_op jit(solution)/shard_map/reshape;reshape | solution.py:39
  241.0 2.7 fusion.9
  243.7 1.2 copy.108
  244.9 2.6 reshape.204
  247.5 4.4 %all-to-all-start.4 = ((bf16[2,16,1,8,1024]{4,1,0,2,3:T(8,128)(2,1)}), bf16[2,16,1,8,1024]{4,1,0,2,3:T(8,128)(2,1)}, u32[]{:S(2)}, u32[]{:S(2)}) async-start(bf16[2,16,1,8,1024]{4,1,0,2,3:T(8,128)(2,1)} %reshape.204), calls=%async_computation.4 | async-start | bytes 1048576 | tf_op jit(solution)/shard_map/all_to_all | solution.py:59
  251.9 2.2 fusion.34
  254.1 3.4 %fusion.39 = (f32[2,8,2,16,8]{4,3,2,1,0:T(8,128)S(1)}, f32[2,8,2,16,8,8]{4,5,3,2,1,0:T(8,128)S(1)}) fusion(f32[16,8,8]{1,2,0:T(8,128)S(1)} %copy.88, bf16[2,8,8,2,1,16,64]{6,5,4,3,2,1,0:T(8,128)(2,1)} %get-tuple-element.7, bf16[2,8,8,2,1,16,64]{6,5,4,3,2,1,0:T(8,128)(2,1)} %get-tuple-element.6), kind=kOutput, calls=%fused_computation.81 | convolution fusion | flops 4325383 | bytes 1200128 | tf_op jit(solution)/shard_map/sub | solution.py:47
  257.6 5.8 %convolution_convert_fusion.2 = bf16[256,3072]{1,0:T(8,128)(2,1)} fusion(bf16[256,1024]{1,0:T(8,128)(2,1)S(1)} %copy-done.8, bf16[1024,3072]{1,0:T(8,128)(2,1)} %bitcast), kind=kOutput, calls=%fused_computation.5 | convolution fusion | flops 1611399168 | bytes 8388608 | tf_op jit(solution)/shard_map/dot_general | solution.py:70
  263.4 0.9 fusion.8
  264.3 0.2 copy.107
  264.5 1.4 reshape.203
  265.9 3.6 %reshape_reshape.9 = bf16[2,64,1,2,3,16,64]{6,5,4,3,1,0,2:T(8,128)(2,1)S(1)} reshape(bf16[256,3072]{1,0:T(8,128)(2,1)} %convolution_convert_fusion.2) | data formatting | bytes 3145728 | tf_op jit(solution)/shard_map/reshape;reshape | solution.py:39
  269.6 2.0 fusion.35
  271.6 2.3 copy.111
  273.9 0.0 all-to-all-done.4
  273.9 4.4 %all-to-all-start.2 = ((bf16[2,8,8,2,1024]{4,3,1,0,2:T(2,128)(2,1)}), bf16[2,8,8,2,1024]{4,3,1,0,2:T(2,128)(2,1)}, u32[]{:S(2)}, u32[]{:S(2)}) async-start(bf16[2,8,8,2,1024]{4,3,1,0,2:T(2,128)(2,1)} %reshape.203), calls=%async_computation.2 | async-start | bytes 1048576 | tf_op jit(solution)/shard_map/all_to_all | solution.py:55
  278.4 3.7 %fusion.38 = (f32[2,2,16,64]{3,2,1,0:T(8,128)S(1)}, f32[2,2,16,64,64]{3,4,2,1,0:T(8,128)}) fusion(f32[16,64,64]{1,2,0:T(8,128)} %copy.81, bf16[2,64,1,2,1,16,64]{6,5,4,3,1,0,2:T(8,128)(2,1)S(1)} %copy-done.4, bf16[2,64,1,2,1,16,64]{6,5,4,3,1,0,2:T(8,128)(2,1)S(1)} %copy-done.5), kind=kOutput, calls=%fused_computation.80 | convolution fusion | flops 34603072 | bytes 2375680 | tf_op jit(solution)/shard_map/sub | solution.py:47
  282.0 3.4 %convert_bitcast_fusion = f32[2,64,1,2,16,64]{1,5,4,3,0,2:T(8,128)} fusion(f32[2,2,16,64,64]{3,4,2,1,0:T(8,128)} %get-tuple-element.17, bf16[2,64,1,2,1,16,64]{1,6,5,3,0,4,2:T(8,128)(2,1)S(1)} %copy.111, f32[2,2,16,64]{3,2,1,0:T(8,128)S(1)} %get-tuple-element.16), kind=kOutput, calls=%fused_computation.6 | convolution fusion | flops 34603008 | bytes 2637824 | tf_op jit(solution)/shard_map/byzhxw,bwyzhs->bxyzhs/dot_general | solution.py:50
  285.4 3.1 %copy.83 = f32[2,64,1,2,16,64]{5,4,3,1,0,2:T(8,128)S(1)} copy(f32[2,64,1,2,16,64]{1,5,4,3,0,2:T(8,128)} %convert_bitcast_fusion) | data formatting | bytes 2097152 | tf_op jit(solution)/shard_map/convert_element_type | solution.py:90
  288.5 0.6 reshape.194
  289.1 1.1 copy.101
  290.2 0.1 convert_bitcast_fusion.1
  290.3 0.8 copy.102
  291.1 1.7 reshape.196
  292.8 0.5 all-to-all-done.2
  293.3 1.5 convert_bitcast_fusion.2
  294.8 0.1 copy.92
  294.8 1.7 reshape.195
  296.6 3.1 %fusion.10 = bf16[256,1024]{1,0:T(8,128)(2,1)S(1)} fusion(f32[256,1024]{1,0:T(8,128)S(1)} %copy-done.3, bf16[1024,1024]{1,0:T(8,128)(2,1)} %all-gather.2.cloned.1.call-done, f32[256,1024]{1,0:T(8,128)} %reshape.196, f32[256,1024]{1,0:T(8,128)S(1)} %reshape.194, f32[256,1024]{1,0:T(8,128)} %reshape.195), kind=kOutput, calls=%fused_computation.28 | convolution fusion | flops 538181632 | bytes 6815744 | tf_op jit(solution)/shard_map/dot_general | solution.py:93
  299.7 1.0 reshape.192
  (23 shorter events, 0.1 us)
Async XLA Ops:
  6.5 49.1 %copy-start = (f32[16,127]{1,0:T(8,128)S(1)}, f32[16,127]{1,0:T(8,128)}, u32[]{:S(2)}) copy-start(f32[16,127]{1,0:T(8,128)} %param.9) | copy-start | bytes 24388
  8.1 36.4 %copy-start.7 = (bf16[128,3072]{1,0:T(8,128)(2,1)S(1)}, bf16[128,3072]{1,0:T(8,128)(2,1)}, u32[]{:S(2)}) copy-start(bf16[128,3072]{1,0:T(8,128)(2,1)} %param.7) | copy-start | bytes 2359300
  47.9 6.0 %copy-start.9 = (f32[16,15]{1,0:T(8,128)S(1)}, f32[16,15]{1,0:T(8,128)}, u32[]{:S(2)}) copy-start(f32[16,15]{1,0:T(8,128)} %param.10) | copy-start | bytes 2884
  47.9 6.3 %copy-start.10 = (f32[16,15]{1,0:T(8,128)S(1)}, f32[16,15]{1,0:T(8,128)}, u32[]{:S(2)}) copy-start(f32[16,15]{1,0:T(8,128)} %param.11) | copy-start | bytes 2884
  47.9 167.4 %all-to-all-start = ((bf16[8,128,3072]{2,1,0:T(8,128)(2,1)}), bf16[8,128,3072]{2,1,0:T(8,128)(2,1)}, u32[]{:S(2)}, u32[]{:S(2)}) async-start(bf16[8,128,3072]{2,1,0:T(8,128)(2,1)} %stack.2), calls=%async_computation | async-start | bytes 12582912 | tf_op jit(solution)/shard_map/all_to_all | solution.py:66
  52.8 243.8 %all-gather.2.cloned.1.call-start = ((), (), s32[]{:S(2)}) async-start(), calls=%async_computation.5 | async-start | bytes 2359296 | tf_op jit(solution)/shard_map/all_gather | solution.py:94
  53.6 6.3 %copy-start.2 = (bf16[2,64,1,2,1024]{4,3,2,1,0:T(2,128)(2,1)S(1)}, bf16[2,64,1,2,1024]{4,3,2,1,0:T(2,128)(2,1)}, u32[]{:S(2)}) copy-start(bf16[2,64,1,2,1024]{4,3,2,1,0:T(2,128)(2,1)} %param.6) | copy-start | bytes 1572868
  247.5 26.4 %all-to-all-start.4 = ((bf16[2,16,1,8,1024]{4,1,0,2,3:T(8,128)(2,1)}), bf16[2,16,1,8,1024]{4,1,0,2,3:T(8,128)(2,1)}, u32[]{:S(2)}, u32[]{:S(2)}) async-start(bf16[2,16,1,8,1024]{4,1,0,2,3:T(8,128)(2,1)} %reshape.204), calls=%async_computation.4 | async-start | bytes 1048576 | tf_op jit(solution)/shard_map/all_to_all | solution.py:59
  254.1 3.4 %copy-start.8 = (bf16[256,1024]{1,0:T(8,128)(2,1)S(1)}, bf16[256,1024]{1,0:T(8,128)(2,1)}, u32[]{:S(2)}) copy-start(bf16[256,1024]{1,0:T(8,128)(2,1)} %reshape.182) | copy-start | bytes 1572868
  257.6 5.9 %copy-start.6 = (bf16[2,8,8,2,1,16,64]{6,5,4,3,2,1,0:T(8,128)(2,1)S(1)}, bf16[2,8,8,2,1,16,64]{6,5,4,3,2,1,0:T(8,128)(2,1)}, u32[]{:S(2)}) copy-start(bf16[2,8,8,2,1,16,64]{6,5,4,3,2,1,0:T(8,128)(2,1)} %get-tuple-element.5) | copy-start | bytes 1572868
  271.6 6.8 %copy-start.4 = (bf16[2,64,1,2,1,16,64]{6,5,4,3,1,0,2:T(8,128)(2,1)S(1)}, bf16[2,64,1,2,1,16,64]{6,5,4,3,1,0,2:T(8,128)(2,1)}, u32[]{:S(2)}) copy-start(bf16[2,64,1,2,1,16,64]{6,5,4,3,1,0,2:T(8,128)(2,1)} %get-tuple-element.9) | copy-start | bytes 1572868
  271.6 6.8 %copy-start.5 = (bf16[2,64,1,2,1,16,64]{6,5,4,3,1,0,2:T(8,128)(2,1)S(1)}, bf16[2,64,1,2,1,16,64]{6,5,4,3,1,0,2:T(8,128)(2,1)}, u32[]{:S(2)}) copy-start(bf16[2,64,1,2,1,16,64]{6,5,4,3,1,0,2:T(8,128)(2,1)} %get-tuple-element.10) | copy-start | bytes 1572868
  273.9 19.3 %all-to-all-start.2 = ((bf16[2,8,8,2,1024]{4,3,1,0,2:T(2,128)(2,1)}), bf16[2,8,8,2,1024]{4,3,1,0,2:T(2,128)(2,1)}, u32[]{:S(2)}, u32[]{:S(2)}) async-start(bf16[2,8,8,2,1024]{4,3,1,0,2:T(2,128)(2,1)} %reshape.203), calls=%async_computation.2 | async-start | bytes 1048576 | tf_op jit(solution)/shard_map/all_to_all | solution.py:55
  294.7 1.8 copy-start.3
  296.6 4.1 %copy-start.1 = (f32[16,127]{1,0:T(8,128)S(1)}, f32[16,127]{1,0:T(8,128)}, u32[]{:S(2)}) copy-start(f32[16,127]{1,0:T(8,128)} %param.9) | copy-start | bytes 24388
Sparse Core Ops, SparseCore 0:
  55.8 135.6 all-gather.1
